TPU v7x, 32 devices: a whole 2x2x4 slice. The times are simulated.
32 devices in a mesh: dp: 8 (over y, x, core), tensor: 4 (over z).
Axes of the slice: x: 2, y: 2, z: 4, core: 2. Of those that a mesh axis runs over, the one named last changes fastest.
Arguments:
- hidden_in: bfloat16 [1024, 2048], P('dp'), may hold values from -6 to 6
- attn_gain: float32 [2048], replicated, may hold values from 0.5 to 1.5
- query_weight: bfloat16 [2048, 2048], P('dp', 'tensor'), may hold values from -0.125 to 0.125
- key_weight: bfloat16 [2048, 2048], P('dp', 'tensor'), may hold values from -0.125 to 0.125
- value_weight: bfloat16 [2048, 2048], P('dp', 'tensor'), may hold values from -0.125 to 0.125
- output_weight: bfloat16 [2048, 2048], P('dp', 'tensor'), may hold values from -1.5 to 1.5
- query_gain: float32 [2048], P('tensor'), may hold values from 0.5 to 1.5
- key_gain: float32 [2048], P('tensor'), may hold values from 0.5 to 1.5
- moe_gain: float32 [2048], replicated, may hold values from 0.5 to 1.5
- expert_gate_up: bfloat16 [2048, 16, 2, 1024], P(None, 'dp', None, 'tensor'), may hold values from -0.125 to 0.125
- expert_down: bfloat16 [2048, 16, 1024], P(None, 'dp', 'tensor'), may hold values from -0.1875 to 0.1875
- experts: int32 [1024, 8], P('dp'), may hold values from 0 to 15, all different within a row
- gates: float32 [1024, 8], P('dp'), may hold values from 0.25 to 0.75
- anchor: int32 [1024], P('dp'), may hold values from 0 to 1023, each once
- lengths: int32 [4], replicated, may hold values from 1 to 512, 1024 in all
- cotangent: bfloat16 [1024, 2048], P('dp'), may hold values from -8 to 8
Outputs:
- output: bfloat16 [1024, 2048], P('dp')
- input_grad: float32 [1024, 2048], P('dp')
- query_grad: float32 [2048, 2048], P('dp', 'tensor')
- key_grad: float32 [2048, 2048], P('dp', 'tensor')
- value_grad: float32 [2048, 2048], P('dp', 'tensor')
- output_grad: float32 [2048, 2048], P('dp', 'tensor')
- gate_up_grad: float32 [2048, 16, 2, 1024], P(None, 'dp', None, 'tensor')
- down_grad: float32 [2048, 16, 1024], P(None, 'dp', 'tensor')
- attn_gain_grad: float32 [2048], P('dp')
- query_gain_grad: float32 [2048], P('dp')
- key_gain_grad: float32 [2048], P('dp')
- moe_gain_grad: float32 [2048], P('dp')
Inputs may be any that keep to these rules, and one draw needn't show every extreme that they name: `anchor`: each number appears once. The lengths sum to 1024; the longest is exactly 512. Each row names 8 different experts.
All inputs are finite; a program needn't handle non-finite values.
Results may differ from a plain program's by a relative error of at most 0.033.
Values may be sent and summed in bfloat16 or wider, within the bound.
A program may use at most 256 MiB of HBM per device.

v0:
```python
import jax
import jax.numpy as jnp
from jax import lax
from jax.sharding import PartitionSpec as P

D = 2048
HD = 128
TOPK = 8
EPSILON = 1e-05
ROPE_BASE = 10000.0
NEG_FILL = -1e30


def rms_norm(values, gain):
    return values * lax.rsqrt(jnp.mean(values * values, axis=-1, keepdims=True) + EPSILON) * gain


def norm_back(values, gain, grad_out):
    inv_rms = lax.rsqrt(jnp.mean(values * values, axis=-1, keepdims=True) + EPSILON)
    weighted = grad_out * gain
    grad_in = inv_rms * weighted - values * inv_rms**3 * jnp.mean(
        weighted * values, axis=-1, keepdims=True
    )
    return (grad_in, jnp.sum(grad_out * values * inv_rms, axis=0))


def locate(anchor, lengths):
    ends = jnp.cumsum(lengths)
    starts = ends - lengths
    docs = jnp.sum((anchor[:, None] >= ends[None, :]).astype(jnp.int32), axis=1)
    which = docs[:, None] == jnp.arange(lengths.shape[0], dtype=jnp.int32)[None, :]
    begins = jnp.sum(jnp.where(which, starts[None, :], 0), axis=1)
    return (docs, (anchor - begins).astype(jnp.int32))


def rotary(tensor, positions):
    half_dim = HD // 2
    freqs = ROPE_BASE ** (-2.0 * jnp.arange(half_dim, dtype=jnp.float32) / HD)
    angles = positions.astype(jnp.float32)[:, None] * freqs[None, :]
    cosine = jnp.cos(angles)[:, None, :]
    sine_part = jnp.sin(angles)[:, None, :]
    first_half = tensor[..., :half_dim]
    second_half = tensor[..., half_dim:]
    return jnp.concatenate(
        [
            first_half * cosine - second_half * sine_part,
            second_half * cosine + first_half * sine_part,
        ],
        axis=-1,
    )


def routing(expert_rows, gate_rows, num_exp, capacity):
    tok_count = expert_rows.shape[0]
    flat_ids = expert_rows.reshape(-1)
    one_hot = (flat_ids[:, None] == jnp.arange(num_exp, dtype=jnp.int32)[None, :]).astype(jnp.int32)
    earlier = jnp.cumsum(one_hot, axis=0) - one_hot
    slot_ids = jnp.sum(earlier * one_hot, axis=1)
    dest_rows = jnp.where(slot_ids < capacity, flat_ids * capacity + slot_ids, num_exp * capacity)
    pair_token = jnp.arange(tok_count * TOPK, dtype=jnp.int32) // TOPK
    slot_source = jnp.zeros((num_exp * capacity + 1,), jnp.int32).at[dest_rows].set(pair_token)
    slot_filled = jnp.zeros((num_exp * capacity + 1,), jnp.float32).at[dest_rows].set(1.0)
    slot_gate = (
        jnp.zeros((num_exp * capacity + 1,), jnp.float32).at[dest_rows].set(gate_rows.reshape(-1))
    )
    return (dest_rows, slot_source[:-1], slot_filled[:-1], slot_gate[:-1])


def pair_allowed(query_anchor, query_docs, key_anchor, key_docs):
    return (
        (query_docs[:, None] == key_docs[None, :]) & (key_anchor[None, :] <= query_anchor[:, None])
    )[None]


def contract_last(left, right):
    return lax.dot_general(
        left, right, (((1,), (1,)), ((), ())), preferred_element_type=jnp.float32
    )


def contract_first(left, right):
    return lax.dot_general(
        left, right, (((0,), (0,)), ((), ())), preferred_element_type=jnp.float32
    )


def shards(
    hidden_in,
    attn_gain,
    query_weight,
    key_weight,
    value_weight,
    output_weight,
    query_gain,
    key_gain,
    moe_gain,
    expert_gate_up,
    expert_down,
    experts,
    gates,
    anchor,
    lengths,
    cotangent,
):
    tok_rows = hidden_in.shape[0]
    head_local = query_weight.shape[1] // HD
    score_scale = HD ** (-0.5)
    f32 = jnp.float32
    bf16 = jnp.bfloat16
    n_dp = lax.axis_size("dp")
    exp_local = expert_down.shape[1]
    num_exp = exp_local * n_dp
    capacity = 9 * tok_rows * TOPK // (8 * num_exp)
    inputs = hidden_in.astype(f32)
    grad_out = cotangent.astype(f32)
    docs, positions = locate(anchor, lengths)
    normed = rms_norm(inputs, attn_gain).astype(bf16)
    query_full, key_full, value_full, output_full = (
        lax.all_gather(query_weight, "dp", axis=0, tiled=True),
        lax.all_gather(key_weight, "dp", axis=0, tiled=True),
        lax.all_gather(value_weight, "dp", axis=0, tiled=True),
        lax.all_gather(output_weight, "dp", axis=0, tiled=True),
    )
    query_raw = jnp.dot(normed, query_full, preferred_element_type=f32)
    key_raw = jnp.dot(normed, key_full, preferred_element_type=f32)
    value_raw = jnp.dot(normed, value_full, preferred_element_type=f32)
    squares = lax.psum(
        (jnp.sum(query_raw * query_raw, axis=1), jnp.sum(key_raw * key_raw, axis=1)), "tensor"
    )
    query_inv = lax.rsqrt(squares[0] / D + EPSILON)[:, None]
    key_inv = lax.rsqrt(squares[1] / D + EPSILON)[:, None]
    query_rows = rotary(
        (query_raw * query_inv * query_gain).reshape(tok_rows, head_local, HD), positions
    ).astype(bf16)
    key_rows = rotary(
        (key_raw * key_inv * key_gain).reshape(tok_rows, head_local, HD), positions
    ).astype(bf16)
    value_rows = value_raw.astype(bf16).reshape(tok_rows, head_local, HD)
    run_max = jnp.full((head_local, tok_rows), NEG_FILL, f32)
    run_acc = jnp.zeros((tok_rows, head_local, HD), f32)
    key_piece = lax.all_gather(key_rows, "dp", axis=0, tiled=True)
    value_piece = lax.all_gather(value_rows, "dp", axis=0, tiled=True)
    anchor_piece = lax.all_gather(anchor, "dp", axis=0, tiled=True)
    piece_docs, unused = locate(anchor_piece, lengths)
    allowed = pair_allowed(anchor, docs, anchor_piece, piece_docs)
    scores = score_scale * jnp.einsum(
        "qhd,khd->hqk", query_rows, key_piece, preferred_element_type=f32
    )
    new_max = jnp.maximum(run_max, jnp.max(jnp.where(allowed, scores, NEG_FILL), axis=2))
    factor = jnp.exp(run_max - new_max)
    attn_probs = jnp.where(allowed, jnp.exp(scores - new_max[:, :, None]), 0.0)
    new_sum = jnp.sum(attn_probs, axis=2)
    update = jnp.einsum(
        "hqk,khd->qhd", attn_probs.astype(bf16), value_piece, preferred_element_type=f32
    )
    run_max, run_sum, run_acc = (new_max, new_sum, run_acc * factor.T[:, :, None] + update)
    log_total = run_max + jnp.log(run_sum)
    attended = run_acc / run_sum.T[:, :, None]
    attended_low = attended.reshape(tok_rows, -1).astype(bf16)
    attn_sum = lax.psum(
        contract_last(attended_low, output_full).astype(jnp.bfloat16), "tensor"
    ).astype(jnp.float32)
    residual = inputs + attn_sum
    moe_in = rms_norm(residual, moe_gain).astype(bf16)
    dest_rows, slot_source, slot_filled, slot_gate = routing(experts, gates, num_exp, capacity)
    buffer_rows = (moe_in[slot_source] * slot_filled[:, None].astype(bf16)).reshape(
        num_exp, capacity, D
    )
    slot_grad = (
        (grad_out[slot_source] * (slot_gate * slot_filled)[:, None])
        .astype(bf16)
        .reshape(num_exp, capacity, D)
    )
    recv_rows, recv_grad = (
        lax.all_to_all(buffer_rows, "dp", split_axis=0, concat_axis=1, tiled=True),
        lax.all_to_all(slot_grad, "dp", split_axis=0, concat_axis=1, tiled=True),
    )
    gate_up = jnp.einsum("ecd,dezf->eczf", recv_rows, expert_gate_up, preferred_element_type=f32)
    gate_part = gate_up[:, :, 0]
    up_part = gate_up[:, :, 1]
    activated = (jax.nn.silu(gate_part) * up_part).astype(bf16)
    expert_out = jnp.einsum("ecf,def->ecd", activated, expert_down, preferred_element_type=f32)
    grad_down = jnp.einsum("ecd,ecf->def", recv_grad, activated, preferred_element_type=f32)
    grad_act = jnp.einsum("ecd,def->ecf", recv_grad, expert_down, preferred_element_type=f32)
    sigmoid_gate = jax.nn.sigmoid(gate_part)
    grad_gate = grad_act * up_part * sigmoid_gate * (1.0 + gate_part * (1.0 - sigmoid_gate))
    grad_up = grad_act * jax.nn.silu(gate_part)
    grad_gateup = jnp.stack([grad_gate, grad_up], axis=2).astype(bf16)
    grad_gateup_w = jnp.einsum("ecd,eczf->dezf", recv_rows, grad_gateup, preferred_element_type=f32)
    grad_buffer = jnp.einsum(
        "eczf,dezf->ecd", grad_gateup, expert_gate_up, preferred_element_type=f32
    )
    back_out, back_grad = (
        lax.all_to_all(
            expert_out.astype(jnp.bfloat16), "dp", split_axis=1, concat_axis=0, tiled=True
        ).astype(expert_out.dtype),
        lax.all_to_all(
            grad_buffer.astype(jnp.bfloat16), "dp", split_axis=1, concat_axis=0, tiled=True
        ).astype(grad_buffer.dtype),
    )
    width = back_out.shape[2]
    zero_row = jnp.zeros((1, width), f32)
    table_rows = jnp.concatenate([back_out.reshape(num_exp * capacity, width), zero_row], axis=0)
    combined = jnp.sum(
        table_rows[dest_rows].reshape(tok_rows, TOPK, width) * gates[:, :, None], axis=1
    )
    grad_table = jnp.concatenate([back_grad.reshape(num_exp * capacity, width), zero_row], axis=0)
    grad_moe_part = jnp.sum(grad_table[dest_rows].reshape(tok_rows, TOPK, width), axis=1)
    moe_sum, grad_moe_in = (
        lax.psum(combined.astype(jnp.bfloat16), "tensor").astype(jnp.float32),
        lax.psum(grad_moe_part.astype(jnp.bfloat16), "tensor").astype(jnp.float32),
    )
    output = (residual + moe_sum).astype(bf16)
    query_full, key_full, value_full, output_full = (
        lax.all_gather(query_weight, "dp", axis=0, tiled=True),
        lax.all_gather(key_weight, "dp", axis=0, tiled=True),
        lax.all_gather(value_weight, "dp", axis=0, tiled=True),
        lax.all_gather(output_weight, "dp", axis=0, tiled=True),
    )
    grad_norm_moe, grad_moe_gain = norm_back(residual, moe_gain, grad_moe_in)
    grad_resid = grad_out + grad_norm_moe
    grad_resid_low = grad_resid.astype(bf16)
    grad_output_w = contract_first(grad_resid_low, attended_low)
    grad_att_low = (
        jnp.dot(grad_resid_low, output_full, preferred_element_type=f32)
        .astype(bf16)
        .reshape(tok_rows, head_local, HD)
    )
    delta_rows = jnp.sum(grad_att_low.astype(f32) * attended, axis=2).T
    key_piece = lax.all_gather(key_rows, "dp", axis=0, tiled=True)
    value_piece = lax.all_gather(value_rows, "dp", axis=0, tiled=True)
    anchor_piece = lax.all_gather(anchor, "dp", axis=0, tiled=True)
    piece_docs, unused = locate(anchor_piece, lengths)
    allowed = pair_allowed(anchor, docs, anchor_piece, piece_docs)
    scores = score_scale * jnp.einsum(
        "qhd,khd->hqk", query_rows, key_piece, preferred_element_type=f32
    )
    attn_probs = jnp.where(allowed, jnp.exp(scores - log_total[:, :, None]), 0.0)
    grad_probs = jnp.einsum("qhd,khd->hqk", grad_att_low, value_piece, preferred_element_type=f32)
    grad_scores = (attn_probs * (grad_probs - delta_rows[:, :, None])).astype(bf16)
    grad_query_rot = score_scale * jnp.einsum(
        "hqk,khd->qhd", grad_scores, key_piece, preferred_element_type=f32
    )
    query_wide = lax.all_gather(
        query_rows.astype(f32).astype(jnp.bfloat16), "dp", axis=0, tiled=True
    ).astype(jnp.float32)
    gradatt_wide = lax.all_gather(
        grad_att_low.astype(f32).astype(jnp.bfloat16), "dp", axis=0, tiled=True
    ).astype(jnp.float32)
    logtot_piece = lax.all_gather(
        log_total.T.astype(jnp.bfloat16), "dp", axis=0, tiled=True
    ).astype(jnp.float32)
    delta_piece = lax.all_gather(
        delta_rows.T.astype(jnp.bfloat16), "dp", axis=0, tiled=True
    ).astype(jnp.float32)
    anchor_piece = lax.all_gather(anchor, "dp", axis=0, tiled=True)
    query_piece = query_wide.astype(bf16)
    gradatt_piece = gradatt_wide.astype(bf16)
    piece_docs, unused = locate(anchor_piece, lengths)
    allowed = pair_allowed(anchor_piece, piece_docs, anchor, docs)
    scores = score_scale * jnp.einsum(
        "qhd,khd->hqk", query_piece, key_rows, preferred_element_type=f32
    )
    attn_probs = jnp.where(allowed, jnp.exp(scores - logtot_piece.T[:, :, None]), 0.0)
    grad_value = jnp.einsum(
        "hqk,qhd->khd", attn_probs.astype(bf16), gradatt_piece, preferred_element_type=f32
    )
    grad_probs = jnp.einsum("qhd,khd->hqk", gradatt_piece, value_rows, preferred_element_type=f32)
    grad_scores = (attn_probs * (grad_probs - delta_piece.T[:, :, None])).astype(bf16)
    grad_key = score_scale * jnp.einsum(
        "hqk,qhd->khd", grad_scores, query_piece, preferred_element_type=f32
    )
    grad_query_hat = rotary(grad_query_rot, -positions).reshape(tok_rows, -1)
    grad_key_hat = rotary(grad_key, -positions).reshape(tok_rows, -1)
    weighted_query = grad_query_hat * query_gain
    weighted_key = grad_key_hat * key_gain
    quarter = query_gain.shape[0]
    gain_offset = lax.axis_index("tensor") * quarter
    query_gain_part = jnp.sum(grad_query_hat * query_raw * query_inv, axis=0)
    key_gain_part = jnp.sum(grad_key_hat * key_raw * key_inv, axis=0)
    query_gain_wide = lax.dynamic_update_slice_in_dim(
        jnp.zeros((D,), f32), query_gain_part, gain_offset, 0
    )
    key_gain_wide = lax.dynamic_update_slice_in_dim(
        jnp.zeros((D,), f32), key_gain_part, gain_offset, 0
    )
    cross = lax.psum(
        (
            jnp.sum(weighted_query * query_raw, axis=1),
            jnp.sum(weighted_key * key_raw, axis=1),
            query_gain_wide,
            key_gain_wide,
        ),
        "tensor",
    )
    grad_query_raw = (
        query_inv * weighted_query - query_raw * query_inv**3 * cross[0][:, None] / D
    ).astype(bf16)
    grad_key_raw = (key_inv * weighted_key - key_raw * key_inv**3 * cross[1][:, None] / D).astype(
        bf16
    )
    grad_value_low = grad_value.reshape(tok_rows, -1).astype(bf16)
    grad_query_w = contract_first(normed, grad_query_raw)
    grad_key_w = contract_first(normed, grad_key_raw)
    grad_value_w = contract_first(normed, grad_value_low)
    grad_normed = (
        contract_last(grad_query_raw, query_full)
        + contract_last(grad_key_raw, key_full)
        + contract_last(grad_value_low, value_full)
    )
    grad_normed_sum = lax.psum(grad_normed.astype(jnp.bfloat16), "tensor").astype(jnp.float32)
    grad_norm_attn, grad_attn_gain = norm_back(inputs, attn_gain, grad_normed_sum)
    input_grad = grad_resid + grad_norm_attn
    summed = (
        lax.psum_scatter(
            grad_query_w.astype(jnp.bfloat16), "dp", scatter_dimension=0, tiled=True
        ).astype(jnp.float32),
        lax.psum_scatter(
            grad_key_w.astype(jnp.bfloat16), "dp", scatter_dimension=0, tiled=True
        ).astype(jnp.float32),
        lax.psum_scatter(
            grad_value_w.astype(jnp.bfloat16), "dp", scatter_dimension=0, tiled=True
        ).astype(jnp.float32),
        lax.psum_scatter(
            grad_output_w.astype(jnp.bfloat16), "dp", scatter_dimension=0, tiled=True
        ).astype(jnp.float32),
        lax.psum_scatter(
            grad_attn_gain.astype(jnp.bfloat16), "dp", scatter_dimension=0, tiled=True
        ).astype(jnp.float32),
        lax.psum_scatter(
            cross[2].astype(jnp.bfloat16), "dp", scatter_dimension=0, tiled=True
        ).astype(jnp.float32),
        lax.psum_scatter(
            cross[3].astype(jnp.bfloat16), "dp", scatter_dimension=0, tiled=True
        ).astype(jnp.float32),
        lax.psum_scatter(
            grad_moe_gain.astype(jnp.bfloat16), "dp", scatter_dimension=0, tiled=True
        ).astype(jnp.float32),
    )
    return (
        output,
        input_grad,
        summed[0],
        summed[1],
        summed[2],
        summed[3],
        grad_gateup_w,
        grad_down,
        summed[4],
        summed[5],
        summed[6],
        summed[7],
    )


def solution(mesh):
    in_specs = (
        P("dp", None),
        P(),
        P("dp", "tensor"),
        P("dp", "tensor"),
        P("dp", "tensor"),
        P("dp", "tensor"),
        P("tensor"),
        P("tensor"),
        P(),
        P(None, "dp", None, "tensor"),
        P(None, "dp", "tensor"),
        P("dp", None),
        P("dp", None),
        P("dp"),
        P(),
        P("dp", None),
    )
    out_specs = (
        P("dp", None),
        P("dp", None),
        P("dp", "tensor"),
        P("dp", "tensor"),
        P("dp", "tensor"),
        P("dp", "tensor"),
        P(None, "dp", None, "tensor"),
        P(None, "dp", "tensor"),
        P("dp"),
        P("dp"),
        P("dp"),
        P("dp"),
    )
    return jax.shard_map(shards, mesh=mesh, in_specs=in_specs, out_specs=out_specs, check_vma=False)
```

profile of v0, /device:TPU:0, one launch (start us, length us, event | category | flops | bytes accessed | tf_op | source)
XLA Modules:
  0.0 867.9 jit_solution(12070746928078635573)
XLA Ops:
  15.4 25.0 %all-gather.10.cloned.1.call-done = bf16[2048,512]{1,0:T(8,128)(2,1)} async-done(((bf16[256,512]{1,0:T(8,128)(2,1)}), bf16[2048,512]{1,0:T(8,128)(2,1)}) %all-gather.10.cloned.1.call-update) | async-done | bytes 2097168 | tf_op jit(solution)/shard_map/all_gather | solution.py:119
  42.8 27.3 %all-gather.12.cloned.1.call-done = bf16[2048,512]{1,0:T(8,128)(2,1)} async-done(((bf16[256,512]{1,0:T(8,128)(2,1)}), bf16[2048,512]{1,0:T(8,128)(2,1)}) %all-gather.12.cloned.1.call-update) | async-done | bytes 2097168 | tf_op jit(solution)/shard_map/all_gather | solution.py:120
  72.3 11.7 %all-reduce.7 = (f32[128]{0:T(128)S(1)}, f32[128]{0:T(128)S(1)}) all-reduce(f32[128]{0:T(128)S(1)} %get-tuple-element.131, f32[128]{0:T(128)S(1)} %get-tuple-element.133), channel_id=1, replica_groups=mesh['dp'=8,'tensor'=4] {'tensor'}, use_global_device_ids=true, to_apply=%region_5.6 | all-reduce | flops 256 | bytes 2048 | tf_op jit(solution)/shard_map/psum | solution.py:127
  93.3 6.6 all-gather.16.cloned.1.call-done
  103.5 4.5 reduce-window.19
  109.0 4.3 scatter_custom_fusion
  113.3 4.3 scatter_custom_fusion.1
  117.7 4.3 scatter_custom_fusion.2
  123.3 6.8 gather_fusion.2
  130.1 6.5 multiply_convert_fusion
  136.6 4.8 all-to-all-start.2
  141.4 65.4 %all-gather = s32[8,1,128]{2,1,0:T(1,128)S(1)} all-gather(s32[1,1,128]{2,1,0:T(1,128)S(1)} %bitcast.187), channel_id=1, replica_groups=mesh['dp'=8,'tensor'=4] {'dp'}, dimensions={0}, use_global_device_ids=true | all-gather | bytes 4608 | tf_op jit(solution)/shard_map/all_gather | solution.py:143
  218.9 38.4 %all-reduce.14.cloned.1.call-done = bf16[128,2048]{1,0:T(8,128)(2,1)} async-done(((bf16[128,2048]{1,0:T(8,128)(2,1)}), bf16[128,2048]{1,0:T(8,128)(2,1)}) %all-reduce.14.cloned.1.call-update) | async-done | bytes 524304 | tf_op jit(solution)/shard_map/psum | solution.py:160
  260.4 5.9 gather_fusion
  266.3 4.9 broadcast_multiply_fusion
  271.2 4.6 all-to-all-start
  275.8 5.3 copy.180
  281.0 49.4 %all-to-all-done = bf16[16,72,2048]{2,1,0:T(8,128)(2,1)} async-done(((bf16[16,72,2048]{2,1,0:T(8,128)(2,1)}), bf16[16,72,2048]{2,1,0:T(8,128)(2,1)}, u32[]{:S(2)}, u32[]{:S(2)}) %all-to-all-start) | async-done | bytes 4718624 | tf_op jit(solution)/shard_map/all_to_all | solution.py:175
  340.2 4.3 bitcast_convert_fusion
  344.5 9.4 %copy.183 = bf16[2,576,2048]{2,0,1:T(2,128)(2,1)} copy(bf16[2,576,2048]{2,1,0:T(8,128)(2,1)} %bitcast_convert_fusion) | data formatting | bytes 9437184 | tf_op jit(solution)/shard_map/convert_element_type | solution.py:198
  353.8 5.0 all-to-all-start.3
  358.9 3.6 convolution_convert_fusion
  362.5 9.3 %copy.176 = bf16[2,576,2048]{2,0,1:T(2,128)(2,1)} copy(bf16[2,576,2048]{2,1,0:T(8,128)(2,1)} %convolution_convert_fusion) | data formatting | bytes 9437184 | tf_op jit(solution)/shard_map/convert_element_type | solution.py:195
  371.8 41.7 %all-to-all-done.3 = bf16[2,576,2048]{2,0,1:T(2,128)(2,1)} async-done(((bf16[2,576,2048]{2,0,1:T(2,128)(2,1)}), bf16[2,576,2048]{2,0,1:T(2,128)(2,1)}, u32[]{:S(2)}, u32[]{:S(2)}) %all-to-all-start.3) | async-done | bytes 4718624 | tf_op jit(solution)/shard_map/all_to_all | solution.py:197
  413.6 4.6 all-to-all-start.1
  419.4 60.7 %all_gather.49 = bf16[1024,4]{0,1:T(4,128)(2,1)S(1)} all-gather(bf16[128,4]{0,1:T(4,128)(2,1)S(1)} %copy-done.64), channel_id=1, replica_groups=mesh['dp'=8,'tensor'=4] {'dp'}, dimensions={0}, use_global_device_ids=true | all-gather | bytes 9216 | tf_op jit(solution)/shard_map/all_gather | solution.py:250
  480.1 4.5 copy.184
  484.6 5.0 pad_convert_fusion
  489.5 12.6 %gather_fusion.3 = f32[1024,2048]{1,0:T(8,128)} fusion(f32[1153,2048]{1,0:T(8,128)} %pad_convert_fusion, s32[1024]{0:T(1024)S(1)} %broadcast_clamp_fusion), kind=kCustom, calls=%fused_computation.3 | custom fusion | bytes 16781312 | tf_op jit(solution)/shard_map/gather | solution.py:208
  502.1 6.2 bitcast_reduce_fusion
  511.7 6.7 copy.177
  518.5 26.7 %all-reduce.16.cloned.1.call-done = bf16[128,2048]{1,0:T(8,128)(2,1)} async-done(((bf16[128,2048]{1,0:T(8,128)(2,1)}), bf16[128,2048]{1,0:T(8,128)(2,1)}) %all-reduce.16.cloned.1.call-update) | async-done | bytes 524304 | tf_op jit(solution)/shard_map/psum | solution.py:211
  550.7 7.3 pad_convert_fusion.1
  557.9 12.6 %gather_fusion.1 = f32[1024,2048]{1,0:T(8,128)} fusion(f32[1153,2048]{1,0:T(8,128)} %pad_convert_fusion.1, s32[1024]{0:T(1024)S(1)} %broadcast_clamp_fusion), kind=kCustom, calls=%fused_computation.1 | custom fusion | bytes 16781312 | tf_op jit(solution)/shard_map/gather | solution.py:205
  570.5 7.5 fusion
  578.1 8.9 %all_gather.51 = bf16[1024,4]{0,1:T(4,128)(2,1)S(1)} all-gather(bf16[128,4]{0,1:T(4,128)(2,1)S(1)} %convert_element_type.256), channel_id=1, replica_groups=mesh['dp'=8,'tensor'=4] {'dp'}, dimensions={0}, use_global_device_ids=true | all-gather | bytes 9216 | tf_op jit(solution)/shard_map/all_gather | solution.py:253
  587.0 3.6 fusion.22
  605.2 19.0 %all-reduce.6 = (f32[128]{0:T(128)}, f32[128]{0:T(128)S(1)}, bf16[2048]{0:T(1024)(128)(2,1)}, bf16[2048]{0:T(1024)(128)(2,1)}) all-reduce(f32[128]{0:T(128)S(1)} %get-tuple-element.79, f32[128]{0:T(128)} %get-tuple-element.77, f32[2048]{0:T(1024)S(1)} %dynamic_update_slice.6, ...), channel_id=1, replica_groups=mesh['dp'=8,'tensor'=4] {'tensor'}, use_global_device_ids=true, to_apply=%region_26.27 | all-reduce | flops 4352 | bytes 26624 | tf_op jit(solution)/shard_map/psum | solution.py:287
  645.2 8.2 convolution_bitcast_fusion
  653.4 13.3 %copy.195 = f32[2048,2,2,256]{3,2,1,0:T(2,128)} copy(f32[2048,2,2,256]{0,3,2,1:T(8,128)} %convolution_bitcast_fusion) | data formatting | bytes 16777216
  666.6 6.2 convolution_bitcast_fusion.1
  672.9 7.2 copy.196
  684.0 24.2 %all-reduce.8 = (bf16[2048]{0:T(1024)(128)(2,1)S(1)}, bf16[2048]{0:T(1024)(128)(2,1)S(1)}, bf16[2048]{0:T(1024)(128)(2,1)S(1)}, bf16[2048]{0:T(1024)(128)(2,1)S(1)}) all-reduce(bf16[2048]{0:T(1024)(128)(2,1)S(1)} %get-tuple-element.74, bf16[2048]{0:T(1024)(128)(2,1)S(1)} %copy-done.65, ...), channel_id=6, replica_groups=mesh['dp'=8,'tensor'=4] {'dp'}, use_global_device_ids=true, to_apply=%region_36.37.clone | all-reduce | flops 8192 | bytes 32768
  710.8 3.7 fusion.24
  714.5 11.6 %reduce-scatter.11.cloned.1.call-done = bf16[256,512]{1,0:T(8,128)(2,1)} async-done(((bf16[2048,512]{1,0:T(8,128)(2,1)}), bf16[256,512]{1,0:T(8,128)(2,1)}) %reduce-scatter.11.cloned.1.call-update) | async-done | bytes 262160 | tf_op jit(solution)/shard_map/reduce_scatter | solution.py:324
  727.9 42.6 %reduce-scatter.9.cloned.1.call-done = bf16[256,512]{1,0:T(8,128)(2,1)} async-done(((bf16[2048,512]{1,0:T(8,128)(2,1)}), bf16[256,512]{1,0:T(8,128)(2,1)}) %reduce-scatter.9.cloned.1.call-update) | async-done | bytes 262160 | tf_op jit(solution)/shard_map/reduce_scatter | solution.py:321
  772.4 42.5 %reduce-scatter.7.cloned.1.call-done = bf16[256,512]{1,0:T(8,128)(2,1)} async-done(((bf16[2048,512]{1,0:T(8,128)(2,1)}), bf16[256,512]{1,0:T(8,128)(2,1)}) %reduce-scatter.7.cloned.1.call-update) | async-done | bytes 262160 | tf_op jit(solution)/shard_map/reduce_scatter | solution.py:318
  816.7 42.5 %reduce-scatter.5.cloned.1.call-done = bf16[256,512]{1,0:T(8,128)(2,1)} async-done(((bf16[2048,512]{1,0:T(8,128)(2,1)}), bf16[256,512]{1,0:T(8,128)(2,1)}) %reduce-scatter.5.cloned.1.call-update) | async-done | bytes 262160 | tf_op jit(solution)/shard_map/reduce_scatter | solution.py:315
  (321 shorter events, 110.5 us)
Async XLA Ops:
  7.2 329.5 %copy-start = (bf16[2048,2,256]{2,1,0:T(2,128)(2,1)S(1)}, bf16[2048,2,256]{2,1,0:T(2,128)(2,1)}, u32[]{:S(2)}) copy-start(bf16[2048,2,256]{2,1,0:T(2,128)(2,1)} %param.26) | copy-start | bytes 6291460
  7.2 33.2 %all-gather.10.cloned.1.call-start = ((), (), s32[]{:S(2)}) async-start(), calls=%async_computation.8 | async-start | bytes 2359296 | tf_op jit(solution)/shard_map/all_gather | solution.py:119
  7.9 62.2 %all-gather.12.cloned.1.call-start = ((), (), s32[]{:S(2)}) async-start(), calls=%async_computation.9 | async-start | bytes 2359296 | tf_op jit(solution)/shard_map/all_gather | solution.py:120
  8.7 61.4 %copy-start.2 = (bf16[128,2048]{1,0:T(8,128)(2,1)S(1)}, bf16[128,2048]{1,0:T(8,128)(2,1)}, u32[]{:S(2)}) copy-start(bf16[128,2048]{1,0:T(8,128)(2,1)} %param.16) | copy-start | bytes 1572868
  8.7 61.4 %copy-start.32 = (f32[2048]{0:T(1024)S(1)}, f32[2048]{0:T(1024)}, u32[]{:S(2)}) copy-start(f32[2048]{0:T(1024)} %param.17) | copy-start | bytes 24580
  8.7 91.1 %all-gather.16.cloned.1.call-start = ((), (), s32[]{:S(2)}) async-start(), calls=%async_computation.11 | async-start | bytes 2359296 | tf_op jit(solution)/shard_map/all_gather | solution.py:121
  9.4 198.1 %all-gather.14.cloned.1.call-start = ((), (), s32[]{:S(2)}) async-start(), calls=%async_computation.10 | async-start | bytes 1179648 | tf_op jit(solution)/shard_map/all_gather | solution.py:141
  15.4 84.4 %copy-start.53 = (f32[128]{0:T(128)}, f32[128]{0:T(128)S(1)}, u32[]{:S(2)}) copy-start(f32[128]{0:T(128)S(1)} %get-tuple-element.122) | copy-start | bytes 1540
  42.8 45.6 %copy-start.14 = (f32[128,512]{1,0:T(8,128)}, f32[128,512]{1,0:T(8,128)S(1)}, u32[]{:S(2)}) copy-start(f32[128,512]{1,0:T(8,128)S(1)} %get-tuple-element.132) | copy-start | bytes 786436
  42.8 42.3 %copy-start.45 = (f32[512]{0:T(512)S(1)}, f32[512]{0:T(512)}, u32[]{:S(2)}) copy-start(f32[512]{0:T(512)} %param.22) | copy-start | bytes 6148
  42.8 44.1 %copy-start.43 = (f32[512]{0:T(512)S(1)}, f32[512]{0:T(512)}, u32[]{:S(2)}) copy-start(f32[512]{0:T(512)} %param.23) | copy-start | bytes 6148
  93.2 118.8 %all-gather.18.cloned.1.call-start = ((), (), s32[]{:S(2)}) async-start(), calls=%async_computation.12 | async-start | bytes 1179648 | tf_op jit(solution)/shard_map/all_gather | solution.py:142
  102.7 112.7 %all-gather.20.cloned.1.call-start = ((), (), s32[]{:S(2)}) async-start(), calls=%async_computation.13 | async-start | bytes 2359296 | tf_op jit(solution)/shard_map/all_gather | solution.py:122
  136.5 70.3 %copy-start.77 = (s32[4,1]{0,1:T(1,128)S(1)}, s32[4,1]{0,1:T(1,128)}, u32[]{:S(2)}) copy-start(s32[4,1]{0,1:T(1,128)} %copy-done.76) | copy-start | bytes 52
  136.5 70.4 %copy-start.71 = (s32[128]{0:T(128)S(1)}, s32[128]{0:T(128)}, u32[]{:S(2)}) copy-start(s32[128]{0:T(128)} %copy-done.70) | copy-start | bytes 1540
  136.5 70.9 %copy-start.26 = (bf16[128,4,64]{2,0,1:T(8,128)(2,1)S(1)}, bf16[128,4,64]{2,0,1:T(8,128)(2,1)}, u32[]{:S(2)}) copy-start(bf16[128,4,64]{2,0,1:T(8,128)(2,1)} %get-tuple-element.109) | copy-start | bytes 196612
  136.5 70.9 %copy-start.27 = (bf16[128,4,64]{2,0,1:T(8,128)(2,1)S(1)}, bf16[128,4,64]{2,0,1:T(8,128)(2,1)}, u32[]{:S(2)}) copy-start(bf16[128,4,64]{2,0,1:T(8,128)(2,1)} %get-tuple-element.110) | copy-start | bytes 196612
  136.6 134.6 %all-to-all-start.2 = ((bf16[16,72,2048]{2,1,0:T(8,128)(2,1)}), bf16[16,72,2048]{2,1,0:T(8,128)(2,1)}, u32[]{:S(2)}, u32[]{:S(2)}) async-start(bf16[16,72,2048]{2,1,0:T(8,128)(2,1)} %multiply_convert_fusion), calls=%async_computation.2 | async-start | bytes 9437184 | tf_op jit(solution)/shard_map/all_to_all | solution.py:176
  141.3 115.9 %all-reduce.14.cloned.1.call-start = ((), (), s32[]{:S(2)}) async-start(), calls=%async_computation.14 | async-start | bytes 1048576 | tf_op jit(solution)/shard_map/psum | solution.py:160
  215.4 43.2 %copy-start.28 = (bf16[128,4,128]{0,2,1:T(8,128)(2,1)}, bf16[128,4,128]{0,2,1:T(8,128)(2,1)S(1)}, u32[]{:S(2)}) copy-start(bf16[128,4,128]{0,2,1:T(8,128)(2,1)S(1)} %get-tuple-element.137) | copy-start | bytes 393220
  215.4 41.9 %copy-start.3 = (bf16[128,2048]{1,0:T(8,128)(2,1)S(1)}, bf16[128,2048]{1,0:T(8,128)(2,1)}, u32[]{:S(2)}) copy-start(bf16[128,2048]{1,0:T(8,128)(2,1)} %param.16) | copy-start | bytes 1572868
  215.4 43.6 %copy-start.34 = (f32[2048]{0:T(1024)S(1)}, f32[2048]{0:T(1024)}, u32[]{:S(2)}) copy-start(f32[2048]{0:T(1024)} %param.24) | copy-start | bytes 24580
  271.2 59.3 %all-to-all-start = ((bf16[16,72,2048]{2,1,0:T(8,128)(2,1)}), bf16[16,72,2048]{2,1,0:T(8,128)(2,1)}, u32[]{:S(2)}, u32[]{:S(2)}) async-start(bf16[16,72,2048]{2,1,0:T(8,128)(2,1)} %broadcast_multiply_fusion), calls=%async_computation | async-start | bytes 9437184 | tf_op jit(solution)/shard_map/all_to_all | solution.py:175
  353.8 59.8 %all-to-all-start.3 = ((bf16[2,576,2048]{2,0,1:T(2,128)(2,1)}), bf16[2,576,2048]{2,0,1:T(2,128)(2,1)}, u32[]{:S(2)}, u32[]{:S(2)}) async-start(bf16[2,576,2048]{2,0,1:T(2,128)(2,1)} %copy.183), calls=%async_computation.3 | async-start | bytes 9437184 | tf_op jit(solution)/shard_map/all_to_all | solution.py:197
  371.8 47.2 %copy-start.52 = (s32[1024,1]{0,1:T(1,128)S(1)}, s32[1024,1]{0,1:T(1,128)}, u32[]{:S(2)}) copy-start(s32[1024,1]{0,1:T(1,128)} %copy-done.51) | copy-start | bytes 12292
  371.8 47.2 %copy-start.38 = (s32[8,1,128]{2,1,0:T(1,128)S(1)}, s32[8,1,128]{2,1,0:T(1,128)}, u32[]{:S(2)}) copy-start(s32[8,1,128]{2,1,0:T(1,128)} %copy-done.37) | copy-start | bytes 12292
  371.8 47.2 %copy-start.40 = (s32[1024]{0:T(1024)S(1)}, s32[1024]{0:T(1024)}, u32[]{:S(2)}) copy-start(s32[1024]{0:T(1024)} %copy-done.39) | copy-start | bytes 12292
  371.8 47.3 %copy-start.61 = (s32[128]{0:T(128)S(1)}, s32[128]{0:T(128)}, u32[]{:S(2)}) copy-start(s32[128]{0:T(128)} %param.29) | copy-start | bytes 1540
  371.8 47.3 %copy-start.72 = (s32[128]{0:T(128)S(1)}, s32[128]{0:T(128)}, u32[]{:S(2)}) copy-start(s32[128]{0:T(128)} %copy-done.70) | copy-start | bytes 1540
  371.8 47.6 %copy-start.64 = (bf16[128,4]{0,1:T(4,128)(2,1)S(1)}, bf16[128,4]{0,1:T(4,128)(2,1)}, u32[]{:S(2)}) copy-start(bf16[128,4]{0,1:T(4,128)(2,1)} %get-tuple-element.113) | copy-start | bytes 3076
  413.6 98.2 %all-to-all-start.1 = ((bf16[2,576,2048]{2,0,1:T(2,128)(2,1)}), bf16[2,576,2048]{2,0,1:T(2,128)(2,1)}, u32[]{:S(2)}, u32[]{:S(2)}) async-start(bf16[2,576,2048]{2,0,1:T(2,128)(2,1)} %copy.176), calls=%async_computation.1 | async-start | bytes 9437184 | tf_op jit(solution)/shard_map/all_to_all | solution.py:194
  418.2 90.2 %all-gather.22.cloned.1.call-start = ((), (), s32[]{:S(2)}) async-start(), calls=%async_computation.16 | async-start | bytes 1179648 | tf_op jit(solution)/shard_map/all_gather | solution.py:244
  419.0 126.2 %all-reduce.16.cloned.1.call-start = ((), (), s32[]{:S(2)}) async-start(), calls=%async_computation.15 | async-start | bytes 1048576 | tf_op jit(solution)/shard_map/psum | solution.py:211
  508.3 82.3 %all-gather.24.cloned.1.call-start = ((), (), s32[]{:S(2)}) async-start(), calls=%async_computation.17 | async-start | bytes 1179648 | tf_op jit(solution)/shard_map/all_gather | solution.py:247
  511.7 33.5 %copy-start.57 = (f32[128]{0:T(128)S(1)}, f32[128]{0:T(128)}, u32[]{:S(2)}) copy-start(f32[128]{0:T(128)} %copy-done.56) | copy-start | bytes 1540
  511.7 35.5 %copy-start.8 = (bf16[128,2048]{1,0:T(8,128)(2,1)S(1)}, bf16[128,2048]{1,0:T(8,128)(2,1)}, u32[]{:S(2)}) copy-start(bf16[128,2048]{1,0:T(8,128)(2,1)} %param.31) | copy-start | bytes 1572868
  511.7 35.5 %copy-start.67 = (f32[128]{0:T(128)S(1)}, f32[128]{0:T(128)}, u32[]{:S(2)}) copy-start(f32[128]{0:T(128)} %get-tuple-element.129) | copy-start | bytes 1540
  550.4 132.2 %all-reduce.18.cloned.1.call-start = ((), (), s32[]{:S(2)}) async-start(), calls=%async_computation.22 | async-start | bytes 2097152 | tf_op jit(solution)/shard_map/psum | solution.py:210
  633.2 92.9 %reduce-scatter.11.cloned.1.call-start = ((), (), s32[]{:S(2)}) async-start(), calls=%async_computation.21 | async-start | bytes 2359296 | tf_op jit(solution)/shard_map/reduce_scatter | solution.py:324
  636.5 134.1 %reduce-scatter.9.cloned.1.call-start = ((), (), s32[]{:S(2)}) async-start(), calls=%async_computation.20 | async-start | bytes 2359296 | tf_op jit(solution)/shard_map/reduce_scatter | solution.py:321
  639.4 175.5 %reduce-scatter.7.cloned.1.call-start = ((), (), s32[]{:S(2)}) async-start(), calls=%async_computation.19 | async-start | bytes 2359296 | tf_op jit(solution)/shard_map/reduce_scatter | solution.py:318
  641.7 217.5 %reduce-scatter.5.cloned.1.call-start = ((), (), s32[]{:S(2)}) async-start(), calls=%async_computation.18 | async-start | bytes 2359296 | tf_op jit(solution)/shard_map/reduce_scatter | solution.py:315
  672.8 38.0 %copy-start.55 = (f32[128]{0:T(128)S(1)}, f32[128]{0:T(128)}, u32[]{:S(2)}) copy-start(f32[128]{0:T(128)} %copy-done.53) | copy-start | bytes 1540
  672.8 38.0 %copy-start.59 = (f32[128]{0:T(128)S(1)}, f32[128]{0:T(128)}, u32[]{:S(2)}) copy-start(f32[128]{0:T(128)} %copy-done.56) | copy-start | bytes 1540
  672.8 38.0 %copy-start.69 = (f32[128]{0:T(128)S(1)}, f32[128]{0:T(128)}, u32[]{:S(2)}) copy-start(f32[128]{0:T(128)} %get-tuple-element.129) | copy-start | bytes 1540
  672.9 38.0 %copy-start.74 = (f32[128]{0:T(128)S(1)}, f32[128]{0:T(128)}, u32[]{:S(2)}) copy-start(f32[128]{0:T(128)} %copy-done.73) | copy-start | bytes 1540
  672.9 38.0 %copy-start.75 = (f32[128]{0:T(128)S(1)}, f32[128]{0:T(128)}, u32[]{:S(2)}) copy-start(f32[128]{0:T(128)} %get-tuple-element.121) | copy-start | bytes 1540
  710.8 150.1 %copy-start.1 = (bf16[2048,2,256]{2,1,0:T(2,128)(2,1)S(1)}, bf16[2048,2,256]{2,1,0:T(2,128)(2,1)}, u32[]{:S(2)}) copy-start(bf16[2048,2,256]{2,1,0:T(2,128)(2,1)} %param.26) | copy-start | bytes 6291460
  (57 other events, 362.6 us)
Sparse Core Ops, SparseCore 0:
  9.9 30.4 all-gather.9
  42.3 27.7 all-gather.11
  72.0 27.7 all-gather.15
  102.2 23.3 all-gather.13
  127.9 26.3 all-gather.17
  156.0 52.6 all-gather.19
  218.9 38.3 all-reduce.13
  420.9 35.1 all-gather.21
  508.5 36.7 all-reduce.15
  550.5 23.2 all-gather.23
  633.3 49.2 all-reduce.17
  685.8 40.3 reduce-scatter.10
  729.4 41.1 reduce-scatter.8
  773.7 41.1 reduce-scatter.6
  818.0 41.1 reduce-scatter.4
where the time goes:
time: 877 us; the launch traced here: 868 us
  waiting for transfers between devices  360 us (41%)
  blocking collectives  190 us (22%)
  local copies, waits for them, and re-layouts  129 us (15%)
  other arithmetic  83.5 us (10%)
  matrix products  69.1 us (8%)
  starting transfers between devices  20.1 us (2%)
  between operations  16.2 us (2%)
    all_gather x1, blocking collectives, shards(): anchor_piece = lax.all_gather(anchor, 'dp', axis=0, tiled=True)  65.4 us
    all_gather x1, blocking collectives, shards(): lax.all_gather(log_total.T.astype(jnp.bfloat16), 'dp', axis=0, tiled=True)  60.7 us
    all_to_all x1, waiting for transfers between devices, shards(): lax.all_to_all(buffer_rows, 'dp', split_axis=0, concat_axis=1, tiled=True)  49.4 us
    reduce_scatter x1, waiting for transfers between devices, shards(): lax.psum_scatter(grad_value_w.astype(jnp.bfloat16), 'dp', scatter_dimensi...  42.6 us
    reduce_scatter x1, waiting for transfers between devices, shards(): lax.psum_scatter(grad_key_w.astype(jnp.bfloat16), 'dp', scatter_dimension...  42.5 us
    reduce_scatter x1, waiting for transfers between devices, shards(): lax.psum_scatter(grad_query_w.astype(jnp.bfloat16), 'dp', scatter_dimensi...  42.5 us
    all_to_all x1, waiting for transfers between devices, shards(): lax.all_to_all(grad_buffer.astype(jnp.bfloat16), 'dp', split_axis=1, conc...  41.7 us
    psum x1, waiting for transfers between devices, shards(): lax.psum(contract_last(attended_low, output_full).astype(jnp.bfloat16), '...  38.4 us
  transfers between devices with their start and end apart: 19, of which 12 were waited for; matrix products, arithmetic and copies ran while one was open for 26% of the time, Pallas kernels for 0%

commit v1 on v0

--- a/solution.py
+++ b/solution.py
@@ -2,6 +2,7 @@
 import jax.numpy as jnp
 from jax import lax
 from jax.sharding import PartitionSpec as P
+from jax.lax import all_gather
 
 D = 2048
 HD = 128
@@ -9,6 +10,10 @@
 EPSILON = 1e-05
 ROPE_BASE = 10000.0
 NEG_FILL = -1e30
+
+
+def meet_positions(field_in):
+    return jnp.sum(all_gather(field_in, "tensor"), axis=0)
 
 
 def rms_norm(values, gain):
@@ -208,7 +213,7 @@
     grad_moe_part = jnp.sum(grad_table[dest_rows].reshape(tok_rows, TOPK, width), axis=1)
     moe_sum, grad_moe_in = (
         lax.psum(combined.astype(jnp.bfloat16), "tensor").astype(jnp.float32),
-        lax.psum(grad_moe_part.astype(jnp.bfloat16), "tensor").astype(jnp.float32),
+        meet_positions(grad_moe_part.astype(jnp.bfloat16)).astype(jnp.float32),
     )
     output = (residual + moe_sum).astype(bf16)
     query_full, key_full, value_full, output_full = (

time: 877 us -> 828 us (0.944)
  blocking collectives: 190 us -> 157 us
  waiting for transfers between devices: 360 us -> 344 us
    all_gather x1, blocking collectives: 60.7 us -> 28.7 us  [shards(): lax.all_gather(log_total.T.astype(jnp.bfloat16), 'dp', axis=0, tiled=True)]
    psum x1 -> x0, waiting for transfers between devices: 26.7 us -> none  [shards(): lax.psum(grad_moe_part.astype(jnp.bfloat16), 'tensor').astype(jnp.float32)]
    unnamed x177 -> x179, local copies, waits for them, and re-layouts: 28.1 us -> 28.1 us
  transfers between devices with their start and end apart: 19 -> 19, of which waited for: 12 -> 12; matrix products, arithmetic and copies ran while one was open for 26% -> 27% of each run, Pallas kernels for 0% -> 0%
where the time goes in v1:
time: 828 us; the launch traced here: 819 us
  waiting for transfers between devices  344 us (42%)
  blocking collectives  157 us (19%)
  local copies, waits for them, and re-layouts  129 us (16%)
  other arithmetic  84.5 us (10%)
  matrix products  68.9 us (8%)
  starting transfers between devices  20.4 us (2%)
  between operations  16.2 us (2%)
    all_gather x1, blocking collectives, shards(): anchor_piece = lax.all_gather(anchor, 'dp', axis=0, tiled=True)  65.4 us
    all_to_all x1, waiting for transfers between devices, shards(): lax.all_to_all(buffer_rows, 'dp', split_axis=0, concat_axis=1, tiled=True)  49.5 us
    all_to_all x1, waiting for transfers between devices, shards(): lax.all_to_all(grad_buffer.astype(jnp.bfloat16), 'dp', split_axis=1, conc...  45.2 us
    reduce_scatter x1, waiting for transfers between devices, shards(): lax.psum_scatter(grad_value_w.astype(jnp.bfloat16), 'dp', scatter_dimensi...  42.6 us
    reduce_scatter x1, waiting for transfers between devices, shards(): lax.psum_scatter(grad_key_w.astype(jnp.bfloat16), 'dp', scatter_dimension...  42.5 us
    reduce_scatter x1, waiting for transfers between devices, shards(): lax.psum_scatter(grad_query_w.astype(jnp.bfloat16), 'dp', scatter_dimensi...  42.5 us
    psum x1, waiting for transfers between devices, shards(): lax.psum(contract_last(attended_low, output_full).astype(jnp.bfloat16), '...  38.4 us
    all_gather x1, blocking collectives, shards(): lax.all_gather(log_total.T.astype(jnp.bfloat16), 'dp', axis=0, tiled=True)  28.7 us
  transfers between devices with their start and end apart: 19, of which 12 were waited for; matrix products, arithmetic and copies ran while one was open for 27% of the time, Pallas kernels for 0%

profile of v1, /device:TPU:0, one launch (start us, length us, event | category | flops | bytes accessed | tf_op | source)
XLA Modules:
  0.0 819.3 jit_solution(13346800134732422109)
XLA Ops:
  15.4 25.0 %all-gather.12.cloned.1.call-done = bf16[2048,512]{1,0:T(8,128)(2,1)} async-done(((bf16[256,512]{1,0:T(8,128)(2,1)}), bf16[2048,512]{1,0:T(8,128)(2,1)}) %all-gather.12.cloned.1.call-update) | async-done | bytes 2097168 | tf_op jit(solution)/shard_map/all_gather | solution.py:124
  42.8 27.3 %all-gather.14.cloned.1.call-done = bf16[2048,512]{1,0:T(8,128)(2,1)} async-done(((bf16[256,512]{1,0:T(8,128)(2,1)}), bf16[2048,512]{1,0:T(8,128)(2,1)}) %all-gather.14.cloned.1.call-update) | async-done | bytes 2097168 | tf_op jit(solution)/shard_map/all_gather | solution.py:125
  72.3 11.7 %all-reduce.7 = (f32[128]{0:T(128)S(1)}, f32[128]{0:T(128)S(1)}) all-reduce(f32[128]{0:T(128)S(1)} %get-tuple-element.131, f32[128]{0:T(128)S(1)} %get-tuple-element.133), channel_id=1, replica_groups=mesh['dp'=8,'tensor'=4] {'tensor'}, use_global_device_ids=true, to_apply=%region_5.6 | all-reduce | flops 256 | bytes 2048 | tf_op jit(solution)/shard_map/psum | solution.py:132
  93.3 6.5 all-gather.18.cloned.1.call-done
  103.5 4.5 reduce-window.19
  109.0 4.3 scatter_custom_fusion
  113.3 4.3 scatter_custom_fusion.1
  117.7 4.3 scatter_custom_fusion.2
  123.3 6.8 gather_fusion.2
  130.1 6.5 multiply_convert_fusion
  136.6 4.8 all-to-all-start.2
  141.4 65.4 %all-gather.1 = s32[8,1,128]{2,1,0:T(1,128)S(1)} all-gather(s32[1,1,128]{2,1,0:T(1,128)S(1)} %bitcast.189), channel_id=1, replica_groups=mesh['dp'=8,'tensor'=4] {'dp'}, dimensions={0}, use_global_device_ids=true | all-gather | bytes 4608 | tf_op jit(solution)/shard_map/all_gather | solution.py:148
  218.9 38.4 %all-reduce.13.cloned.1.call-done = bf16[128,2048]{1,0:T(8,128)(2,1)} async-done(((bf16[128,2048]{1,0:T(8,128)(2,1)}), bf16[128,2048]{1,0:T(8,128)(2,1)}) %all-reduce.13.cloned.1.call-update) | async-done | bytes 524304 | tf_op jit(solution)/shard_map/psum | solution.py:165
  260.3 5.9 gather_fusion
  266.3 4.9 broadcast_multiply_fusion
  271.2 4.6 all-to-all-start
  275.8 5.3 copy.180
  281.0 49.5 %all-to-all-done = bf16[16,72,2048]{2,1,0:T(8,128)(2,1)} async-done(((bf16[16,72,2048]{2,1,0:T(8,128)(2,1)}), bf16[16,72,2048]{2,1,0:T(8,128)(2,1)}, u32[]{:S(2)}, u32[]{:S(2)}) %all-to-all-start) | async-done | bytes 4718624 | tf_op jit(solution)/shard_map/all_to_all | solution.py:180
  340.2 4.3 bitcast_convert_fusion
  344.5 9.4 %copy.183 = bf16[2,576,2048]{2,0,1:T(2,128)(2,1)} copy(bf16[2,576,2048]{2,1,0:T(8,128)(2,1)} %bitcast_convert_fusion) | data formatting | bytes 9437184 | tf_op jit(solution)/shard_map/convert_element_type | solution.py:203
  353.8 4.8 all-to-all-start.3
  359.4 3.6 convolution_convert_fusion
  363.0 9.3 %copy.176 = bf16[2,576,2048]{2,0,1:T(2,128)(2,1)} copy(bf16[2,576,2048]{2,1,0:T(8,128)(2,1)} %convolution_convert_fusion) | data formatting | bytes 9437184 | tf_op jit(solution)/shard_map/convert_element_type | solution.py:200
  372.3 45.2 %all-to-all-done.3 = bf16[2,576,2048]{2,0,1:T(2,128)(2,1)} async-done(((bf16[2,576,2048]{2,0,1:T(2,128)(2,1)}), bf16[2,576,2048]{2,0,1:T(2,128)(2,1)}, u32[]{:S(2)}, u32[]{:S(2)}) %all-to-all-start.3) | async-done | bytes 4718624 | tf_op jit(solution)/shard_map/all_to_all | solution.py:202
  417.5 4.6 all-to-all-start.1
  422.4 4.5 copy.184
  426.9 5.0 pad_convert_fusion
  431.8 12.6 %gather_fusion.3 = f32[1024,2048]{1,0:T(8,128)} fusion(f32[1153,2048]{1,0:T(8,128)} %pad_convert_fusion, s32[1024]{0:T(1024)S(1)} %broadcast_clamp_fusion), kind=kCustom, calls=%fused_computation.3 | custom fusion | bytes 16781312 | tf_op jit(solution)/shard_map/gather | solution.py:213
  444.4 6.2 bitcast_reduce_fusion
  451.1 28.7 %all_gather.54 = bf16[1024,4]{0,1:T(4,128)(2,1)S(1)} all-gather(bf16[128,4]{0,1:T(4,128)(2,1)S(1)} %copy-done.65), channel_id=1, replica_groups=mesh['dp'=8,'tensor'=4] {'dp'}, dimensions={0}, use_global_device_ids=true | all-gather | bytes 9216 | tf_op jit(solution)/shard_map/all_gather | solution.py:255
  483.2 6.7 copy.177
  489.9 6.8 all-gather.28.cloned.1.call-done
  503.0 7.3 pad_convert_fusion.1
  510.3 12.6 %gather_fusion.1 = f32[1024,2048]{1,0:T(8,128)} fusion(f32[1153,2048]{1,0:T(8,128)} %pad_convert_fusion.1, s32[1024]{0:T(1024)S(1)} %broadcast_clamp_fusion), kind=kCustom, calls=%fused_computation.1 | custom fusion | bytes 16781312 | tf_op jit(solution)/shard_map/gather | solution.py:210
  522.8 7.5 fusion
  530.4 8.9 %all_gather.56 = bf16[1024,4]{0,1:T(4,128)(2,1)S(1)} all-gather(bf16[128,4]{0,1:T(4,128)(2,1)S(1)} %convert_element_type.269), channel_id=1, replica_groups=mesh['dp'=8,'tensor'=4] {'dp'}, dimensions={0}, use_global_device_ids=true | all-gather | bytes 9216 | tf_op jit(solution)/shard_map/all_gather | solution.py:258
  539.3 3.6 fusion.22
  557.5 18.1 %all-reduce.6 = (f32[128]{0:T(128)}, f32[128]{0:T(128)S(1)}, bf16[2048]{0:T(1024)(128)(2,1)}, bf16[2048]{0:T(1024)(128)(2,1)}) all-reduce(f32[128]{0:T(128)S(1)} %get-tuple-element.79, f32[128]{0:T(128)} %get-tuple-element.77, f32[2048]{0:T(1024)S(1)} %dynamic_update_slice.6, ...), channel_id=1, replica_groups=mesh['dp'=8,'tensor'=4] {'tensor'}, use_global_device_ids=true, to_apply=%region_26.27 | all-reduce | flops 4352 | bytes 26624 | tf_op jit(solution)/shard_map/psum | solution.py:292
  596.6 8.2 convolution_bitcast_fusion
  604.8 13.3 %copy.195 = f32[2048,2,2,256]{3,2,1,0:T(2,128)} copy(f32[2048,2,2,256]{0,3,2,1:T(8,128)} %convolution_bitcast_fusion) | data formatting | bytes 16777216
  618.0 6.2 convolution_bitcast_fusion.1
  624.3 7.2 copy.196
  635.4 24.2 %all-reduce.8 = (bf16[2048]{0:T(1024)(128)(2,1)S(1)}, bf16[2048]{0:T(1024)(128)(2,1)S(1)}, bf16[2048]{0:T(1024)(128)(2,1)S(1)}, bf16[2048]{0:T(1024)(128)(2,1)S(1)}) all-reduce(bf16[2048]{0:T(1024)(128)(2,1)S(1)} %get-tuple-element.74, bf16[2048]{0:T(1024)(128)(2,1)S(1)} %copy-done.66, ...), channel_id=7, replica_groups=mesh['dp'=8,'tensor'=4] {'dp'}, use_global_device_ids=true, to_apply=%region_36.37.clone | all-reduce | flops 8192 | bytes 32768
  662.3 3.7 fusion.24
  665.9 11.6 %reduce-scatter.11.cloned.1.call-done = bf16[256,512]{1,0:T(8,128)(2,1)} async-done(((bf16[2048,512]{1,0:T(8,128)(2,1)}), bf16[256,512]{1,0:T(8,128)(2,1)}) %reduce-scatter.11.cloned.1.call-update) | async-done | bytes 262160 | tf_op jit(solution)/shard_map/reduce_scatter | solution.py:329
  679.4 42.6 %reduce-scatter.9.cloned.1.call-done = bf16[256,512]{1,0:T(8,128)(2,1)} async-done(((bf16[2048,512]{1,0:T(8,128)(2,1)}), bf16[256,512]{1,0:T(8,128)(2,1)}) %reduce-scatter.9.cloned.1.call-update) | async-done | bytes 262160 | tf_op jit(solution)/shard_map/reduce_scatter | solution.py:326
  723.8 42.5 %reduce-scatter.7.cloned.1.call-done = bf16[256,512]{1,0:T(8,128)(2,1)} async-done(((bf16[2048,512]{1,0:T(8,128)(2,1)}), bf16[256,512]{1,0:T(8,128)(2,1)}) %reduce-scatter.7.cloned.1.call-update) | async-done | bytes 262160 | tf_op jit(solution)/shard_map/reduce_scatter | solution.py:323
  768.1 42.5 %reduce-scatter.5.cloned.1.call-done = bf16[256,512]{1,0:T(8,128)(2,1)} async-done(((bf16[2048,512]{1,0:T(8,128)(2,1)}), bf16[256,512]{1,0:T(8,128)(2,1)}) %reduce-scatter.5.cloned.1.call-update) | async-done | bytes 262160 | tf_op jit(solution)/shard_map/reduce_scatter | solution.py:320
  (324 shorter events, 111.7 us)
Async XLA Ops:
  7.2 329.5 %copy-start = (bf16[2048,2,256]{2,1,0:T(2,128)(2,1)S(1)}, bf16[2048,2,256]{2,1,0:T(2,128)(2,1)}, u32[]{:S(2)}) copy-start(bf16[2048,2,256]{2,1,0:T(2,128)(2,1)} %param.26) | copy-start | bytes 6291460
  7.2 33.2 %all-gather.12.cloned.1.call-start = ((), (), s32[]{:S(2)}) async-start(), calls=%async_computation.8 | async-start | bytes 2359296 | tf_op jit(solution)/shard_map/all_gather | solution.py:124
  7.9 62.2 %all-gather.14.cloned.1.call-start = ((), (), s32[]{:S(2)}) async-start(), calls=%async_computation.9 | async-start | bytes 2359296 | tf_op jit(solution)/shard_map/all_gather | solution.py:125
  8.7 61.4 %copy-start.2 = (bf16[128,2048]{1,0:T(8,128)(2,1)S(1)}, bf16[128,2048]{1,0:T(8,128)(2,1)}, u32[]{:S(2)}) copy-start(bf16[128,2048]{1,0:T(8,128)(2,1)} %param.16) | copy-start | bytes 1572868
  8.7 61.4 %copy-start.33 = (f32[2048]{0:T(1024)S(1)}, f32[2048]{0:T(1024)}, u32[]{:S(2)}) copy-start(f32[2048]{0:T(1024)} %param.17) | copy-start | bytes 24580
  8.7 91.1 %all-gather.18.cloned.1.call-start = ((), (), s32[]{:S(2)}) async-start(), calls=%async_computation.11 | async-start | bytes 2359296 | tf_op jit(solution)/shard_map/all_gather | solution.py:126
  9.4 198.1 %all-gather.16.cloned.1.call-start = ((), (), s32[]{:S(2)}) async-start(), calls=%async_computation.10 | async-start | bytes 1179648 | tf_op jit(solution)/shard_map/all_gather | solution.py:146
  15.4 84.4 %copy-start.54 = (f32[128]{0:T(128)}, f32[128]{0:T(128)S(1)}, u32[]{:S(2)}) copy-start(f32[128]{0:T(128)S(1)} %get-tuple-element.122) | copy-start | bytes 1540
  42.8 45.6 %copy-start.15 = (f32[128,512]{1,0:T(8,128)}, f32[128,512]{1,0:T(8,128)S(1)}, u32[]{:S(2)}) copy-start(f32[128,512]{1,0:T(8,128)S(1)} %get-tuple-element.132) | copy-start | bytes 786436
  42.8 42.3 %copy-start.46 = (f32[512]{0:T(512)S(1)}, f32[512]{0:T(512)}, u32[]{:S(2)}) copy-start(f32[512]{0:T(512)} %param.22) | copy-start | bytes 6148
  42.8 44.2 %copy-start.44 = (f32[512]{0:T(512)S(1)}, f32[512]{0:T(512)}, u32[]{:S(2)}) copy-start(f32[512]{0:T(512)} %param.23) | copy-start | bytes 6148
  72.3 19.4 %copy-start.17 = (f32[128,512]{1,0:T(8,128)}, f32[128,512]{1,0:T(8,128)S(1)}, u32[]{:S(2)}) copy-start(f32[128,512]{1,0:T(8,128)S(1)} %get-tuple-element.134) | copy-start | bytes 786436
  93.3 15.5 %copy-start.64 = (f32[128,8]{0,1:T(8,128)S(1)}, f32[128,8]{0,1:T(8,128)}, u32[]{:S(2)}) copy-start(f32[128,8]{0,1:T(8,128)} %param.28) | copy-start | bytes 12292
  93.3 118.7 %all-gather.20.cloned.1.call-start = ((), (), s32[]{:S(2)}) async-start(), calls=%async_computation.12 | async-start | bytes 1179648 | tf_op jit(solution)/shard_map/all_gather | solution.py:147
  102.7 112.7 %all-gather.22.cloned.1.call-start = ((), (), s32[]{:S(2)}) async-start(), calls=%async_computation.13 | async-start | bytes 2359296 | tf_op jit(solution)/shard_map/all_gather | solution.py:127
  136.5 70.3 %copy-start.78 = (s32[4,1]{0,1:T(1,128)S(1)}, s32[4,1]{0,1:T(1,128)}, u32[]{:S(2)}) copy-start(s32[4,1]{0,1:T(1,128)} %copy-done.77) | copy-start | bytes 52
  136.5 70.4 %copy-start.72 = (s32[128]{0:T(128)S(1)}, s32[128]{0:T(128)}, u32[]{:S(2)}) copy-start(s32[128]{0:T(128)} %copy-done.71) | copy-start | bytes 1540
  136.5 70.9 %copy-start.27 = (bf16[128,4,64]{2,0,1:T(8,128)(2,1)S(1)}, bf16[128,4,64]{2,0,1:T(8,128)(2,1)}, u32[]{:S(2)}) copy-start(bf16[128,4,64]{2,0,1:T(8,128)(2,1)} %get-tuple-element.109) | copy-start | bytes 196612
  136.6 70.9 %copy-start.28 = (bf16[128,4,64]{2,0,1:T(8,128)(2,1)S(1)}, bf16[128,4,64]{2,0,1:T(8,128)(2,1)}, u32[]{:S(2)}) copy-start(bf16[128,4,64]{2,0,1:T(8,128)(2,1)} %get-tuple-element.110) | copy-start | bytes 196612
  136.6 134.6 %all-to-all-start.2 = ((bf16[16,72,2048]{2,1,0:T(8,128)(2,1)}), bf16[16,72,2048]{2,1,0:T(8,128)(2,1)}, u32[]{:S(2)}, u32[]{:S(2)}) async-start(bf16[16,72,2048]{2,1,0:T(8,128)(2,1)} %multiply_convert_fusion), calls=%async_computation.2 | async-start | bytes 9437184 | tf_op jit(solution)/shard_map/all_to_all | solution.py:181
  141.3 115.9 %all-reduce.13.cloned.1.call-start = ((), (), s32[]{:S(2)}) async-start(), calls=%async_computation.14 | async-start | bytes 1048576 | tf_op jit(solution)/shard_map/psum | solution.py:165
  215.4 43.2 %copy-start.29 = (bf16[128,4,128]{0,2,1:T(8,128)(2,1)}, bf16[128,4,128]{0,2,1:T(8,128)(2,1)S(1)}, u32[]{:S(2)}) copy-start(bf16[128,4,128]{0,2,1:T(8,128)(2,1)S(1)} %get-tuple-element.137) | copy-start | bytes 393220
  215.4 41.9 %copy-start.3 = (bf16[128,2048]{1,0:T(8,128)(2,1)S(1)}, bf16[128,2048]{1,0:T(8,128)(2,1)}, u32[]{:S(2)}) copy-start(bf16[128,2048]{1,0:T(8,128)(2,1)} %param.16) | copy-start | bytes 1572868
  215.4 43.6 %copy-start.35 = (f32[2048]{0:T(1024)S(1)}, f32[2048]{0:T(1024)}, u32[]{:S(2)}) copy-start(f32[2048]{0:T(1024)} %param.24) | copy-start | bytes 24580
  271.2 59.3 %all-to-all-start = ((bf16[16,72,2048]{2,1,0:T(8,128)(2,1)}), bf16[16,72,2048]{2,1,0:T(8,128)(2,1)}, u32[]{:S(2)}, u32[]{:S(2)}) async-start(bf16[16,72,2048]{2,1,0:T(8,128)(2,1)} %broadcast_multiply_fusion), calls=%async_computation | async-start | bytes 9437184 | tf_op jit(solution)/shard_map/all_to_all | solution.py:180
  339.2 20.2 %copy-start.13 = (bf16[2,576,256]{2,1,0:T(8,128)(2,1)}, bf16[2,576,256]{2,1,0:T(8,128)(2,1)S(1)}, u32[]{:S(2)}) copy-start(bf16[2,576,256]{2,1,0:T(8,128)(2,1)S(1)} %get-tuple-element.94) | copy-start | bytes 1769476
  353.8 63.7 %all-to-all-start.3 = ((bf16[2,576,2048]{2,0,1:T(2,128)(2,1)}), bf16[2,576,2048]{2,0,1:T(2,128)(2,1)}, u32[]{:S(2)}, u32[]{:S(2)}) async-start(bf16[2,576,2048]{2,0,1:T(2,128)(2,1)} %copy.183), calls=%async_computation.3 | async-start | bytes 9437184 | tf_op jit(solution)/shard_map/all_to_all | solution.py:202
  358.6 121.3 %all-gather.24.cloned.1.call-start = ((), (), s32[]{:S(2)}) async-start(), calls=%async_computation.15 | async-start | bytes 1179648 | tf_op jit(solution)/shard_map/all_gather | solution.py:249
  417.5 65.6 %all-to-all-start.1 = ((bf16[2,576,2048]{2,0,1:T(2,128)(2,1)}), bf16[2,576,2048]{2,0,1:T(2,128)(2,1)}, u32[]{:S(2)}, u32[]{:S(2)}) async-start(bf16[2,576,2048]{2,0,1:T(2,128)(2,1)} %copy.176), calls=%async_computation.1 | async-start | bytes 9437184 | tf_op jit(solution)/shard_map/all_to_all | solution.py:199
  422.2 74.5 %all-gather.28.cloned.1.call-start = ((), (), s32[]{:S(2)}) async-start(), calls=%async_computation.21 | async-start | bytes 2621440 | tf_op jit(solution)/shard_map/all_gather | solution.py:16
  444.4 35.5 %copy-start.43 = (f32[4,128]{1,0:T(4,128)S(1)}, f32[4,128]{1,0:T(4,128)}, u32[]{:S(2)}) copy-start(f32[4,128]{1,0:T(4,128)} %copy-done.42) | copy-start | bytes 6148
  444.4 35.4 %copy-start.49 = (f32[4,128]{1,0:T(4,128)S(1)}, f32[4,128]{1,0:T(4,128)}, u32[]{:S(2)}) copy-start(f32[4,128]{1,0:T(4,128)} %copy-done.48) | copy-start | bytes 6148
  444.4 35.5 %copy-start.26 = (bf16[128,4,128]{2,0,1:T(8,128)(2,1)S(1)}, bf16[128,4,128]{2,0,1:T(8,128)(2,1)}, u32[]{:S(2)}) copy-start(bf16[128,4,128]{2,0,1:T(8,128)(2,1)} %pad_maximum_fusion.4) | copy-start | bytes 393220
  450.7 92.3 %all-gather.26.cloned.1.call-start = ((), (), s32[]{:S(2)}) async-start(), calls=%async_computation.16 | async-start | bytes 1179648 | tf_op jit(solution)/shard_map/all_gather | solution.py:252
  502.8 131.3 %all-reduce.15.cloned.1.call-start = ((), (), s32[]{:S(2)}) async-start(), calls=%async_computation.22 | async-start | bytes 2097152 | tf_op jit(solution)/shard_map/psum | solution.py:215
  522.8 16.4 %copy-start.6 = (f32[4,128,1024]{2,1,0:T(8,128)S(1)}, f32[4,128,1024]{2,1,0:T(8,128)}, u32[]{:S(2)}) copy-start(f32[4,128,1024]{2,1,0:T(8,128)} %copy-done.5) | copy-start | bytes 6291460
  548.1 29.9 %copy-start.7 = (f32[4,1024,128]{2,1,0:T(8,128)S(1)}, f32[4,1024,128]{2,1,0:T(8,128)}, u32[]{:S(2)}) copy-start(f32[4,1024,128]{2,1,0:T(8,128)} %exponential_select_fusion) | copy-start | bytes 6291460
  584.6 93.0 %reduce-scatter.11.cloned.1.call-start = ((), (), s32[]{:S(2)}) async-start(), calls=%async_computation.20 | async-start | bytes 2359296 | tf_op jit(solution)/shard_map/reduce_scatter | solution.py:329
  587.9 134.1 %reduce-scatter.9.cloned.1.call-start = ((), (), s32[]{:S(2)}) async-start(), calls=%async_computation.19 | async-start | bytes 2359296 | tf_op jit(solution)/shard_map/reduce_scatter | solution.py:326
  590.8 175.5 %reduce-scatter.7.cloned.1.call-start = ((), (), s32[]{:S(2)}) async-start(), calls=%async_computation.18 | async-start | bytes 2359296 | tf_op jit(solution)/shard_map/reduce_scatter | solution.py:323
  593.1 217.5 %reduce-scatter.5.cloned.1.call-start = ((), (), s32[]{:S(2)}) async-start(), calls=%async_computation.17 | async-start | bytes 2359296 | tf_op jit(solution)/shard_map/reduce_scatter | solution.py:320
  604.8 13.3 %copy-start.14 = (bf16[2,576,256]{2,1,0:T(8,128)(2,1)S(1)}, bf16[2,576,256]{2,1,0:T(8,128)(2,1)}, u32[]{:S(2)}) copy-start(bf16[2,576,256]{2,1,0:T(8,128)(2,1)} %copy-done.13) | copy-start | bytes 1769476
  624.2 38.0 %copy-start.56 = (f32[128]{0:T(128)S(1)}, f32[128]{0:T(128)}, u32[]{:S(2)}) copy-start(f32[128]{0:T(128)} %copy-done.54) | copy-start | bytes 1540
  624.2 38.0 %copy-start.60 = (f32[128]{0:T(128)S(1)}, f32[128]{0:T(128)}, u32[]{:S(2)}) copy-start(f32[128]{0:T(128)} %copy-done.57) | copy-start | bytes 1540
  624.2 38.0 %copy-start.70 = (f32[128]{0:T(128)S(1)}, f32[128]{0:T(128)}, u32[]{:S(2)}) copy-start(f32[128]{0:T(128)} %get-tuple-element.129) | copy-start | bytes 1540
  624.3 38.0 %copy-start.75 = (f32[128]{0:T(128)S(1)}, f32[128]{0:T(128)}, u32[]{:S(2)}) copy-start(f32[128]{0:T(128)} %copy-done.74) | copy-start | bytes 1540
  624.3 38.0 %copy-start.76 = (f32[128]{0:T(128)S(1)}, f32[128]{0:T(128)}, u32[]{:S(2)}) copy-start(f32[128]{0:T(128)} %get-tuple-element.121) | copy-start | bytes 1540
  662.3 150.1 %copy-start.1 = (bf16[2048,2,256]{2,1,0:T(2,128)(2,1)S(1)}, bf16[2048,2,256]{2,1,0:T(2,128)(2,1)}, u32[]{:S(2)}) copy-start(bf16[2048,2,256]{2,1,0:T(2,128)(2,1)} %param.26) | copy-start | bytes 6291460
  (58 other events, 259.7 us)
Sparse Core Ops, SparseCore 0:
  9.9 30.4 all-gather.11
  42.3 27.7 all-gather.13
  72.0 27.7 all-gather.17
  102.2 23.3 all-gather.15
  127.9 26.3 all-gather.19
  156.0 52.6 all-gather.21
  218.9 38.3 all-reduce.12
  361.3 35.1 all-gather.23
  450.8 45.8 all-gather.27
  502.9 22.2 all-gather.25
  584.7 49.2 all-reduce.14
  637.2 40.3 reduce-scatter.10
  680.8 41.1 reduce-scatter.8
  725.1 41.1 reduce-scatter.6
  769.4 41.1 reduce-scatter.4
